TPU v7x, 16 devices: a whole 2x2x2 slice. The times are simulated.
16 devices in a mesh: data: 2 (over z), tp: 8 (over y, x, core).
Axes of the slice: x: 2, y: 2, z: 2, core: 2. Of those that a mesh axis runs over, the one named last changes fastest.
Arguments:
- X: bfloat16 [8192, 3072], P(('data', 'tp')), parts along dimension 0
- gamma: float32 [3072], replicated
- W1: bfloat16 [3072, 8192], P(None, 'tp')
- W2: bfloat16 [8192, 3072], P('tp')
- dY: bfloat16 [8192, 3072], P(('data', 'tp')), parts along dimension 0
Outputs:
- output 1: bfloat16 [8192, 3072], P(('data', 'tp')), parts along dimension 0
- output 2: bfloat16 [8192, 3072], P(('data', 'tp')), parts along dimension 0
- output 3: float32 [6144, 8192], P('data', 'tp'), parts along dimension 0
- output 4: float32 [16384, 3072], P(('data', 'tp')), parts along dimension 0
- output 5: float32 [6144], P('data'), parts along dimension 0
There are 2 independent parts. A program takes and returns all parts, laid end to end along the dimension named above; an argument that names none is the same for every part.
All inputs are finite; a program needn't handle non-finite values.
Results may differ from a plain program's by a relative error of at most 0.001.
Values are sent between devices in bfloat16 or wider.
A program may use at most 1 GiB of HBM per device.

v0:
```python
import jax
import jax.numpy as jnp
from jax import lax
from jax.sharding import PartitionSpec as P

EPS = 1e-6


def _gelu(a):
    return jax.nn.gelu(a, approximate=True)


def _ln(x):
    mu = jnp.mean(x, axis=-1, keepdims=True)
    xc = x - mu
    var = jnp.mean(xc * xc, axis=-1, keepdims=True)
    rstd = lax.rsqrt(var + EPS)
    return xc * rstd, rstd


def _tn(a, b):
    return lax.dot_general(a, b, (((0,), (0,)), ((), ())), preferred_element_type=jnp.float32)


def _nt(a, b):
    return lax.dot_general(a, b, (((1,), (1,)), ((), ())), preferred_element_type=jnp.float32)


def solution(mesh):
    rows = P(("data", "tp"), None)

    def body(X, gamma, W1, W2, dY):
        x = X.astype(jnp.float32)
        xhatv, rstd = _ln(x)
        Xn = lax.all_gather((xhatv * gamma).astype(jnp.bfloat16), "tp", axis=0, tiled=True)
        A = jnp.dot(Xn, W1, preferred_element_type=jnp.float32)
        H = _gelu(A).astype(jnp.bfloat16)
        Yp = jnp.dot(H, W2, preferred_element_type=jnp.float32)
        Y = (x + lax.psum_scatter(Yp, "tp", scatter_dimension=0, tiled=True)).astype(jnp.bfloat16)
        g = lax.all_gather(dY, "tp", axis=0, tiled=True)
        dW2 = _tn(H, g)
        dH = _nt(g, W2)
        dA = jax.vjp(_gelu, A)[1](dH)[0].astype(jnp.bfloat16)
        dW1 = _tn(Xn, dA)
        dXn = lax.psum_scatter(_nt(dA, W1), "tp", scatter_dimension=0, tiled=True)
        dgamma = lax.psum(jnp.sum(dXn * xhatv, axis=0), "tp")
        dxhat = dXn * gamma
        dx = rstd * (dxhat - jnp.mean(dxhat, axis=-1, keepdims=True) - xhatv * jnp.mean(dxhat * xhatv, axis=-1, keepdims=True))
        dX = (dY.astype(jnp.float32) + dx).astype(jnp.bfloat16)
        return Y, dX, dW1, dW2, dgamma

    return jax.shard_map(body, mesh=mesh,
                         in_specs=(rows, P(None), P(None, "tp"), P("tp", None), rows),
                         out_specs=(rows, rows, P("data", "tp"), rows, P("data")),
                         check_vma=False)
```

profile of v0, /device:TPU:0, one launch (start us, length us, event | category | flops | bytes accessed | tf_op | source)
XLA Modules:
  0.0 911.3 jit_solution(4187184061796407351)
XLA Ops:
  7.2 0.0 all-gather.5.cloned.1.call-start
  7.2 0.7 all-gather.5.cloned.1.call-update
  7.9 0.0 all-gather.3.cloned.1.call-start
  7.9 2.4 convert_reduce_fusion
  10.3 2.8 fusion.20
  13.2 0.6 copy-done.4
  13.8 5.2 fusion.13
  19.0 0.0 all-gather.3.cloned.1.call-update
  19.1 0.6 reduce-scatter.5.cloned.1.call-start
  19.6 114.5 %all-gather.5.cloned.1.call-done = bf16[4096,3072]{1,0:T(8,128)(2,1)} async-done(((bf16[512,3072]{1,0:T(8,128)(2,1)}), bf16[4096,3072]{1,0:T(8,128)(2,1)}) %all-gather.5.cloned.1.call-update) | async-done | bytes 25165840 | tf_op jit(solution)/shard_map/all_gather | solution.py:40
  134.1 33.3 %fusion.24 = f32[4096,1024]{1,0:T(8,128)} fusion(bf16[4096,3072]{1,0:T(8,128)(2,1)} %all-gather.5.cloned.1.call-done, bf16[1024,3072]{1,0:T(8,128)(2,1)} %param.8), kind=kOutput, calls=%fused_computation.35 | convolution fusion | flops 25769803776 | bytes 48234496 | tf_op jit(solution)/shard_map/dot_general | solution.py:26
  167.5 90.6 %all-gather.3.cloned.1.call-done = bf16[4096,3072]{1,0:T(8,128)(2,1)} async-done(((bf16[512,3072]{1,0:T(8,128)(2,1)}), bf16[4096,3072]{1,0:T(8,128)(2,1)}) %all-gather.3.cloned.1.call-update) | async-done | bytes 25165840 | tf_op jit(solution)/shard_map/all_gather | solution.py:35
  258.0 42.7 %fusion.6 = (bf16[4096,1024]{1,0:T(8,128)(2,1)S(1)}, f32[4096,1024]{1,0:T(8,128)}) fusion(f32[4096,1024]{1,0:T(8,128)} %fusion.24, bf16[4096,3072]{1,0:T(8,128)(2,1)} %all-gather.3.cloned.1.call-done, bf16[3072,1024]{1,0:T(8,128)(2,1)} %param.7), kind=kOutput, calls=%fused_computation.8 | convolution fusion | flops 25853689856 | bytes 73400320 | tf_op jit(solution)/shard_map/dot_general | solution.py:36
  300.8 3.2 copy-done.6
  304.0 33.3 %fusion.25 = f32[4096,3072]{1,0:T(8,128)} fusion(bf16[4096,1024]{1,0:T(8,128)(2,1)S(1)} %get-tuple-element.10, bf16[3072,1024]{1,0:T(8,128)(2,1)} %param.7), kind=kOutput, calls=%fused_computation.36 | convolution fusion | flops 25769803776 | bytes 65011712 | tf_op jit(solution)/shard_map/dot_general | solution.py:26
  337.3 0.0 reduce-scatter.3.cloned.1.call-start
  337.3 36.5 %fusion.23 = f32[4096,3072]{1,0:T(8,128)} fusion(bf16[1024,3072]{1,0:T(8,128)(2,1)} %param.8, f32[4096,1024]{1,0:T(8,128)} %get-tuple-element.11), kind=kOutput, calls=%fused_computation.34 | convolution fusion | flops 25807552512 | bytes 73400320 | tf_op jit(solution)/shard_map/dot_general | solution.py:38
  373.8 43.1 %fusion.22 = f32[1024,3072]{1,0:T(8,128)} fusion(bf16[4096,3072]{1,0:T(8,128)(2,1)} %all-gather.5.cloned.1.call-done, f32[4096,1024]{1,0:T(8,128)} %get-tuple-element.11), kind=kOutput, calls=%fused_computation.33 | convolution fusion | flops 25807552512 | bytes 54525952 | tf_op jit(solution)/shard_map/dot_general | solution.py:22
  417.0 34.3 %fusion.26 = f32[3072,1024]{1,0:T(8,128)} fusion(bf16[4096,3072]{1,0:T(8,128)(2,1)} %all-gather.3.cloned.1.call-done, bf16[4096,1024]{1,0:T(8,128)(2,1)} %copy-done.6), kind=kOutput, calls=%fused_computation.37 | convolution fusion | flops 25769803776 | bytes 46137344 | tf_op jit(solution)/shard_map/dot_general | solution.py:22
  451.2 163.5 %reduce-scatter.5.cloned.1.call-done = f32[512,3072]{1,0:T(8,128)} async-done(((f32[4096,3072]{1,0:T(8,128)}), f32[512,3072]{1,0:T(8,128)}) %reduce-scatter.5.cloned.1.call-update) | async-done | bytes 6291472 | tf_op jit(solution)/shard_map/reduce_scatter | solution.py:45
  614.7 4.5 fusion.19
  619.2 22.8 %psum.7 = f32[3072]{0:T(1024)} all-reduce(f32[3072]{0:T(1024)S(1)} %get-tuple-element.5), channel_id=1, replica_groups=mesh['data'=2,'tp'=8] {'tp'}, use_global_device_ids=true, to_apply=%region_7.0 | all-reduce | flops 3072 | bytes 24576 | tf_op jit(solution)/shard_map/psum | solution.py:46
  642.0 253.4 %reduce-scatter.3.cloned.1.call-done = f32[512,3072]{1,0:T(8,128)} async-done(((f32[4096,3072]{1,0:T(8,128)}), f32[512,3072]{1,0:T(8,128)}) %reduce-scatter.3.cloned.1.call-update) | async-done | bytes 6291472 | tf_op jit(solution)/shard_map/reduce_scatter | solution.py:39
  895.4 9.1 fusion.18
  (17 shorter events, 0.1 us)
Async XLA Ops:
  7.2 127.0 %all-gather.5.cloned.1.call-start = ((), (), s32[]{:S(2)}) async-start(), calls=%async_computation.4 | async-start | bytes 28311552 | tf_op jit(solution)/shard_map/all_gather | solution.py:40
  7.9 250.1 %all-gather.3.cloned.1.call-start = ((), (), s32[]{:S(2)}) async-start(), calls=%async_computation.2 | async-start | bytes 28311552 | tf_op jit(solution)/shard_map/all_gather | solution.py:35
  10.3 2.9 copy-start.2
  13.2 0.6 copy-start.4
  19.1 595.6 %reduce-scatter.5.cloned.1.call-start = ((), (), s32[]{:S(2)}) async-start(), calls=%async_computation.5 | async-start | bytes 56623104 | tf_op jit(solution)/shard_map/reduce_scatter | solution.py:45
  300.8 3.2 copy-start.6
  337.3 558.1 %reduce-scatter.3.cloned.1.call-start = ((), (), s32[]{:S(2)}) async-start(), calls=%async_computation.3 | async-start | bytes 56623104 | tf_op jit(solution)/shard_map/reduce_scatter | solution.py:39
  416.9 197.8 %copy-start = (bf16[512,3072]{1,0:T(8,128)(2,1)S(1)}, bf16[512,3072]{1,0:T(8,128)(2,1)}, u32[]{:S(2)}) copy-start(bf16[512,3072]{1,0:T(8,128)(2,1)} %param.5) | copy-start | bytes 9437188
  416.9 197.8 %copy-start.1 = (f32[3072]{0:T(1024)S(1)}, f32[3072]{0:T(1024)}, u32[]{:S(2)}) copy-start(f32[3072]{0:T(1024)} %param.6) | copy-start | bytes 36868
  416.9 197.8 %copy-start.3 = (f32[512]{0:T(512)S(1)}, f32[512]{0:T(512)}, u32[]{:S(2)}) copy-start(f32[512]{0:T(512)} %copy-done.2) | copy-start | bytes 6148
  417.0 197.8 %copy-start.5 = (f32[512]{0:T(512)S(1)}, f32[512]{0:T(512)}, u32[]{:S(2)}) copy-start(f32[512]{0:T(512)} %copy-done.4) | copy-start | bytes 6148
Sparse Core Ops, SparseCore 0:
  9.8 124.2 all-gather.4
  136.5 121.4 all-gather.2
  337.4 277.2 reduce-scatter.4
  618.1 277.2 reduce-scatter.2
where the time goes:
time: 914 us; the launch traced here: 911 us
  waiting for transfers between devices  623 us (68%)
  matrix products  223 us (24%)
  other arithmetic  24 us (3%)
  blocking collectives  22.8 us (2%)
  between operations  14.1 us (2%)
    reduce_scatter x1, waiting for transfers between devices, body(): lax.psum_scatter(Yp, 'tp', scatter_dimension=0, tiled=True)  253 us
    reduce_scatter x1, waiting for transfers between devices, body(): dXn = lax.psum_scatter(_nt(dA, W1), 'tp', scatter_dimension=0, tiled=True)  163 us
    all_gather x1, waiting for transfers between devices, body(): g = lax.all_gather(dY, 'tp', axis=0, tiled=True)  115 us
    all_gather x1, waiting for transfers between devices, body(): lax.all_gather((xhatv * gamma).astype(jnp.bfloat16), 'tp', axis=0, tiled=...  90.6 us
    dot_general x2, matrix products, _tn(): lax.dot_general(a, b, (((0,), (0,)), ((), ())), preferred_element_type=jn...  77.4 us
    dot_general x2, matrix products, _nt(): lax.dot_general(a, b, (((1,), (1,)), ((), ())), preferred_element_type=jn...  66.6 us
    dot_general x1, matrix products, body(): A = jnp.dot(Xn, W1, preferred_element_type=jnp.float32)  42.7 us
    dot_general x1, matrix products, body(): Yp = jnp.dot(H, W2, preferred_element_type=jnp.float32)  36.5 us
  transfers between devices with their start and end apart: 4, of which 4 were waited for; matrix products, arithmetic and copies ran while one was open for 18% of the time, Pallas kernels for 0%

commit v1 on v0

v1 whole, which is shorter than its diff:
```python
import jax
import jax.numpy as jnp
from jax import lax
from jax.sharding import PartitionSpec as P


EPS = 1e-6
BF = jnp.bfloat16
F32 = jnp.float32


def _gelu(a):
    return jax.nn.gelu(a, approximate=True)


def _ln(x):
    mu = jnp.mean(x, axis=-1, keepdims=True)
    xc = x - mu
    var = jnp.mean(xc * xc, axis=-1, keepdims=True)
    rstd = lax.rsqrt(var + EPS)
    return xc * rstd, rstd


def _nn(a, b):
    return jnp.dot(a, b, preferred_element_type=F32)


def _tn(a, b):
    return lax.dot_general(a, b, (((0,), (0,)), ((), ())), preferred_element_type=F32)


def _nt(a, b):
    return lax.dot_general(a, b, (((1,), (1,)), ((), ())), preferred_element_type=F32)


def _swap(bit):
    return lambda v: lax.ppermute(v, "tp", [(i, i ^ bit) for i in range(8)])


CORE, XN, YN = _swap(1), _swap(2), _swap(4)


def ZN(v):
    return lax.ppermute(v, "data", [(0, 1), (1, 0)])


def _dact(A, dH):
    return jax.vjp(_gelu, A)[1](dH)[0].astype(BF)


def _cat(*v):
    return jnp.concatenate(v)


tie = lambda *v: lax.optimization_barrier(v)


def solution(mesh):
    rows = P(("data", "tp"), None)

    def block(X, gamma, W1, W2, dY):
        n = X.shape[0]
        zi = lax.axis_index("data")
        half = W2.shape[0] // 2
        q = half // 2
        W1T = W1.T

        def piece(w, c):
            return lax.dynamic_slice_in_dim(w, zi * half + c * q, q, 0)

        def group(Xnc, dYc, w1, w2, Yp, dXp):
            Ak = _nt(Xnc, w1)
            Yp = Yp + _nn(_gelu(Ak).astype(BF), w2)
            dXp = dXp + _nn(_dact(Ak, _nt(dYc, w2)), w1)
            return Yp, dXp

        Xp, dYp = CORE(X), CORE(dY)
        a1, a2 = piece(W1T, 0), piece(W2, 0)
        x1, y1, x2, y2 = XN(a1), YN(a1), XN(a2), YN(a2)
        Xs, a1, a2 = tie(X, a1, a2)
        x = Xs.astype(F32)
        xhat, rstd = _ln(x)
        Xn = (xhat * gamma).astype(BF)
        Xa = lax.all_gather(Xn, "tp", axis=0, tiled=True)
        dYs, W1s, W2s, Xn, Xp, dYp = tie(dY, W1T, W2, Xn, Xp, dYp)
        g = lax.all_gather(dYs, "tp", axis=0, tiled=True)
        b1, b2 = piece(W1s, 1), piece(W2s, 1)
        bx1, by1, bx2, by2 = XN(b1), YN(b1), XN(b2), YN(b2)
        b1, b2, Xp = tie(b1, b2, Xp)
        Xnc = _cat(Xn, (_ln(Xp.astype(F32))[0] * gamma).astype(BF))
        dYc = _cat(dY, dYp)

        A0 = _nn(Xnc, W1)
        dA0 = _dact(A0, _nt(dYc, W2))
        x1, y1, A0, dA0 = tie(x1, y1, A0, dA0)
        zx1, zy1, d1 = ZN(x1), ZN(y1), XN(y1)
        P0, Q0 = _nn(_gelu(A0).astype(BF), W2), _nt(dA0, W1)
        x2, y2, P0, Q0 = tie(x2, y2, P0, Q0)
        zx2, zy2, d2 = ZN(x2), ZN(y2), YN(x2)

        Xa, P0, Q0 = tie(Xa, P0, Q0)
        A = _nn(Xa, W1)
        d1, d2, bx1, by1, bx2, by2, A = tie(d1, d2, bx1, by1, bx2, by2, A)
        zd1, zd2 = ZN(d1), ZN(d2)
        bzx1, bzy1, bzx2, bzy2 = ZN(bx1), ZN(by1), ZN(bx2), ZN(by2)
        bd1, bd2 = XN(by1), YN(bx2)
        g, A = tie(g, A)
        dA = _dact(A, _nt(g, W2))
        bd1, bd2, dA, gs = tie(bd1, bd2, dA, g)
        bzd1, bzd2 = ZN(bd1), ZN(bd2)
        dW2 = _tn(_gelu(A).astype(BF), gs)
        zx1, zy1, zx2, zy2, zd1, zd2, dW2 = tie(zx1, zy1, zx2, zy2, zd1, zd2, dW2)
        P1, Q1 = group(Xnc, dYc, _cat(x1, y1, d1, zx1, zy1, zd1), _cat(x2, y2, d2, zx2, zy2, zd2), P0, Q0)
        P1, Q1, dA = tie(P1, Q1, dA)
        dW1 = _tn(Xa, dA)
        bzx1, bzy1, bzx2, bzy2, bzd1, bzd2, dW1 = tie(bzx1, bzy1, bzx2, bzy2, bzd1, bzd2, dW1)
        Yp, dXp = group(Xnc, dYc, _cat(bx1, by1, bd1, bzx1, bzy1, bzd1), _cat(bx2, by2, bd2, bzx2, bzy2, bzd2), P1, Q1)

        dXn = dXp[:n] + CORE(dXp[n:])
        Y = (x + (Yp[:n] + CORE(Yp[n:]))).astype(BF)
        dgamma = jnp.sum(dXn * xhat, axis=0)
        for hop in (CORE, XN, YN):
            dgamma = dgamma + hop(dgamma)
        dxhat = dXn * gamma
        dx = rstd * (dxhat - jnp.mean(dxhat, axis=-1, keepdims=True) - xhat * jnp.mean(dxhat * xhat, axis=-1, keepdims=True))
        dX = (dY.astype(F32) + dx).astype(BF)
        return Y, dX, dW1, dW2, dgamma

    return jax.shard_map(block, mesh=mesh,
                         in_specs=(rows, P(None), P(None, "tp"), P("tp", None), rows),
                         out_specs=(rows, rows, P("data", "tp"), rows, P("data")),
                         check_vma=False)
```

time: 914 us -> 910 us (level)
  waiting for transfers between devices: 623 us -> 423 us
  matrix products: 223 us -> 332 us
  local copies, waits for them, and re-layouts: 3.79 us -> 80.6 us
  starting transfers between devices: 0.68 us -> 31.9 us
  blocking collectives: 22.8 us -> 0 us
    reduce_scatter x2 -> x0, waiting for transfers between devices: 417 us -> none  [the longest x1 253 us: body(): lax.psum_scatter(Yp, 'tp', scatter_dimension=0, tiled=True)]
    ppermute x0 -> x31, waiting for transfers between devices: none -> 305 us  [the longest x19 176 us: _swap(): return lambda v: lax.ppermute(v, 'tp', [(i, i ^ bit) for i in range(8)])]
    dot_general x6 -> x16, matrix products: 223 us -> 332 us  [the longest x7 137 us: _nn(): return jnp.dot(a, b, preferred_element_type=F32)]
    all_gather x2, waiting for transfers between devices: 205 us -> 118 us  [the longest x1 79.8 us: block(): g = lax.all_gather(dYs, 'tp', axis=0, tiled=True)]
    unnamed x14 -> x87, local copies, waits for them, and re-layouts: 3.79 us -> 56.1 us
    ppermute x0 -> x31, starting transfers between devices: none -> 31.3 us  [the longest x19 18.2 us: _swap(): return lambda v: lax.ppermute(v, 'tp', [(i, i ^ bit) for i in range(8)])]
    psum x1 -> x0, blocking collectives: 22.8 us -> none  [body(): dgamma = lax.psum(jnp.sum(dXn * xhatv, axis=0), 'tp')]
    dynamic_slice x0 -> x4, local copies, waits for them, and re-layouts: none -> 11 us  [piece(): return lax.dynamic_slice_in_dim(w, zi * half + c * q, q, 0)]
  transfers between devices with their start and end apart: 4 -> 33, of which waited for: 4 -> 15; matrix products, arithmetic and copies ran while one was open for 18% -> 39% of each run, Pallas kernels for 0% -> 0%
where the time goes in v1:
time: 910 us; the launch traced here: 907 us
  waiting for transfers between devices  423 us (46%)
  matrix products  332 us (36%)
  local copies, waits for them, and re-layouts  80.6 us (9%)
  starting transfers between devices  31.9 us (4%)
  other arithmetic  24.3 us (3%)
  between operations  14.6 us (2%)
    ppermute x19, waiting for transfers between devices, _swap(): return lambda v: lax.ppermute(v, 'tp', [(i, i ^ bit) for i in range(8)])  176 us
    dot_general x7, matrix products, _nn(): return jnp.dot(a, b, preferred_element_type=F32)  137 us
    ppermute x12, waiting for transfers between devices, ZN(): return lax.ppermute(v, 'data', [(0, 1), (1, 0)])  129 us
    dot_general x7, matrix products, _nt(): lax.dot_general(a, b, (((1,), (1,)), ((), ())), preferred_element_type=F32)  118 us
    all_gather x1, waiting for transfers between devices, block(): g = lax.all_gather(dYs, 'tp', axis=0, tiled=True)  79.8 us
    dot_general x2, matrix products, _tn(): lax.dot_general(a, b, (((0,), (0,)), ((), ())), preferred_element_type=F32)  77.3 us
    unnamed x87, local copies, waits for them, and re-layouts  56.1 us
    all_gather x1, waiting for transfers between devices, block(): Xa = lax.all_gather(Xn, 'tp', axis=0, tiled=True)  38.4 us
  transfers between devices with their start and end apart: 33, of which 15 were waited for; matrix products, arithmetic and copies ran while one was open for 39% of the time, Pallas kernels for 0%

profile of v1, /device:TPU:0, one launch (start us, length us, event | category | flops | bytes accessed | tf_op | source)
XLA Modules:
  0.0 906.6 jit_solution(3428288101357447483)
XLA Ops:
  59.1 11.2 %fusion.52 = bf16[1024,1024]{1,0:T(8,128)(2,1)S(1)} fusion(f32[1024,1024]{1,0:T(8,128)S(1)} %fusion.91, bf16[1024,3072]{1,0:T(8,128)(2,1)S(1)} %constant_dynamic-update-slice_fusion, bf16[1024,3072]{1,0:T(8,128)(2,1)} %param.8), kind=kOutput, calls=%fused_computation.77 | convolution fusion | flops 6463422464 | bytes 18874368 | tf_op jit(solution)/shard_map/dot_general | solution.py:33
  70.3 94.0 %collective-permute-done.2 = bf16[256,3072]{0,1:T(8,128)(2,1)} collective-permute-done((bf16[256,3072]{0,1:T(8,128)(2,1)}, bf16[256,3072]{0,1:T(8,128)(2,1)}, u32[]{:S(2)}, u32[]{:S(2)}) %collective-permute-start.2) | collective-permute-done | bytes 1572896 | tf_op jit(solution)/shard_map/ppermute | solution.py:37
  175.8 12.7 %fusion.83 = f32[1024,3072]{1,0:T(8,128)} fusion(bf16[1024,3072]{1,0:T(8,128)(2,1)} %param.8, f32[1024,1024]{1,0:T(8,128)S(1)} %fusion.91), kind=kOutput, calls=%fused_computation.106 | convolution fusion | flops 6451888128 | bytes 23068672 | tf_op jit(solution)/shard_map/dot_general | solution.py:25
  201.1 38.4 %all-gather.3.cloned.1.call-done = bf16[4096,3072]{1,0:T(8,128)(2,1)} async-done(((bf16[512,3072]{1,0:T(8,128)(2,1)}), bf16[4096,3072]{1,0:T(8,128)(2,1)}) %all-gather.3.cloned.1.call-update) | async-done | bytes 25165840 | tf_op jit(solution)/shard_map/all_gather | solution.py:84
  239.5 44.7 %collective-permute-done.6 = bf16[256,3072]{0,1:T(8,128)(2,1)} collective-permute-done((bf16[256,3072]{0,1:T(8,128)(2,1)}, bf16[256,3072]{0,1:T(8,128)(2,1)}, u32[]{:S(2)}, u32[]{:S(2)}) %collective-permute-start.6) | collective-permute-done | bytes 1572896 | tf_op jit(solution)/shard_map/ppermute | solution.py:37
  285.8 33.4 %fusion.124 = f32[4096,1024]{1,0:T(8,128)} fusion(bf16[4096,3072]{1,0:T(8,128)(2,1)} %all-gather.3.cloned.1.call-done, bf16[3072,1024]{1,0:T(8,128)(2,1)} %param.7), kind=kOutput, calls=%fused_computation.182 | convolution fusion | flops 25769803776 | bytes 48234496 | tf_op jit(solution)/shard_map/dot_general | solution.py:25
  322.7 22.9 %collective-permute-done.10 = bf16[256,3072]{1,0:T(8,128)(2,1)} collective-permute-done((bf16[256,3072]{1,0:T(8,128)(2,1)}, bf16[256,3072]{1,0:T(8,128)(2,1)}, u32[]{:S(2)}, u32[]{:S(2)}) %collective-permute-start.10) | collective-permute-done | bytes 1572896 | tf_op jit(solution)/shard_map/ppermute | solution.py:37
  360.4 79.8 %all-gather.5.cloned.1.call-done = bf16[4096,3072]{1,0:T(8,128)(2,1)} async-done(((bf16[512,3072]{1,0:T(8,128)(2,1)}), bf16[4096,3072]{1,0:T(8,128)(2,1)}) %all-gather.5.cloned.1.call-update) | async-done | bytes 25165840 | tf_op jit(solution)/shard_map/all_gather | solution.py:86
  440.2 42.6 %fusion.6 = bf16[4096,1024]{1,0:T(8,128)(2,1)} fusion(f32[4096,1024]{1,0:T(8,128)} %fusion.124, bf16[4096,3072]{1,0:T(8,128)(2,1)} %all-gather.5.cloned.1.call-done, bf16[1024,3072]{1,0:T(8,128)(2,1)} %param.8), kind=kOutput, calls=%fused_computation.8 | convolution fusion | flops 25853689856 | bytes 56623104 | tf_op jit(solution)/shard_map/dot_general | solution.py:33
  486.3 43.5 %fusion.7 = f32[1024,3072]{1,0:T(8,128)} fusion(bf16[4096,3072]{1,0:T(8,128)(2,1)} %all-gather.5.cloned.1.call-done, f32[4096,1024]{1,0:T(8,128)} %fusion.124), kind=kOutput, calls=%fused_computation.17 | convolution fusion | flops 25807552512 | bytes 54525952 | tf_op jit(solution)/shard_map/dot_general | solution.py:29
  532.4 21.7 %collective-permute-done.16 = bf16[256,3072]{0,1:T(8,128)(2,1)} collective-permute-done((bf16[256,3072]{0,1:T(8,128)(2,1)}, bf16[256,3072]{0,1:T(8,128)(2,1)}, u32[]{:S(2)}, u32[]{:S(2)}) %collective-permute-start.16) | collective-permute-done | bytes 1572896 | tf_op jit(solution)/shard_map/ppermute | solution.py:44
  555.6 32.2 %collective-permute-done.17 = bf16[256,3072]{1,0:T(8,128)(2,1)} collective-permute-done((bf16[256,3072]{1,0:T(8,128)(2,1)}, bf16[256,3072]{1,0:T(8,128)(2,1)}, u32[]{:S(2)}, u32[]{:S(2)}) %collective-permute-start.17) | collective-permute-done | bytes 1572896 | tf_op jit(solution)/shard_map/ppermute | solution.py:44
  596.3 13.9 %fusion.90 = f32[1024,1536]{1,0:T(8,128)} fusion(bf16[1536,3072]{0,1:T(8,128)(2,1)} %constant_dynamic-update-slice_fusion.2, bf16[512,3072]{1,0:T(8,128)(2,1)S(1)} %copy-done.8, bf16[512,3072]{1,0:T(8,128)(2,1)S(1)} %copy-done.6), kind=kOutput, calls=%fused_computation.112 | convolution fusion | flops 9676259328 | bytes 22020096 | tf_op jit(solution)/shard_map/dot_general | solution.py:33
  618.1 13.7 %fusion.125 = f32[1024,1536]{1,0:T(8,128)} fusion(bf16[1024,3072]{1,0:T(8,128)(2,1)S(1)} %bitcast.27, bf16[1536,3072]{1,0:T(8,128)(2,1)} %constant_dynamic-update-slice_fusion.8), kind=kOutput, calls=%fused_computation.183 | convolution fusion | flops 9663676416 | bytes 22020096 | tf_op jit(solution)/shard_map/dot_general | solution.py:33
  631.8 21.9 %convolution_add_fusion.2 = f32[1024,3072]{1,0:T(8,128)} fusion(f32[1024,3072]{1,0:T(8,128)} %fusion.123, bf16[1536,3072]{0,1:T(8,128)(2,1)} %constant_dynamic-update-slice_fusion.2, f32[1024,1536]{1,0:T(8,128)} %fusion.90, f32[1024,1536]{1,0:T(8,128)} %fusion.125), kind=kOutput, calls=%fused_computation.68 | convolution fusion | flops 9698279424 | bytes 47185920 | tf_op jit(solution)/shard_map/dot_general | solution.py:25
  653.7 20.2 %convolution_add_fusion.3 = f32[1024,3072]{1,0:T(8,128)} fusion(f32[1024,3072]{1,0:T(8,128)} %fusion.83, bf16[1536,3072]{1,0:T(8,128)(2,1)} %constant_dynamic-update-slice_fusion.8, f32[1024,1536]{1,0:T(8,128)} %fusion.90), kind=kOutput, calls=%fused_computation.69 | convolution fusion | flops 9680977920 | bytes 40894464 | tf_op jit(solution)/shard_map/dot_general | solution.py:25
  676.0 33.9 %fusion.126 = f32[3072,1024]{1,0:T(8,128)} fusion(bf16[4096,3072]{1,0:T(8,128)(2,1)} %all-gather.3.cloned.1.call-done, bf16[4096,1024]{1,0:T(8,128)(2,1)} %fusion.6), kind=kOutput, calls=%fused_computation.184 | convolution fusion | flops 25769803776 | bytes 46137344 | tf_op jit(solution)/shard_map/dot_general | solution.py:29
  722.7 33.6 %collective-permute-done.24 = bf16[256,3072]{0,1:T(8,128)(2,1)S(1)} collective-permute-done((bf16[256,3072]{0,1:T(8,128)(2,1)}, bf16[256,3072]{0,1:T(8,128)(2,1)S(1)}, u32[]{:S(2)}, u32[]{:S(2)}) %collective-permute-start.24) | collective-permute-done | bytes 1572896 | tf_op jit(solution)/shard_map/ppermute | solution.py:44
  756.3 33.0 %collective-permute-done.25 = bf16[256,3072]{1,0:T(8,128)(2,1)S(1)} collective-permute-done((bf16[256,3072]{1,0:T(8,128)(2,1)}, bf16[256,3072]{1,0:T(8,128)(2,1)S(1)}, u32[]{:S(2)}, u32[]{:S(2)}) %collective-permute-start.25) | collective-permute-done | bytes 1572896 | tf_op jit(solution)/shard_map/ppermute | solution.py:44
  792.6 13.6 %fusion.89 = f32[1024,1536]{1,0:T(8,128)} fusion(bf16[1536,3072]{0,1:T(8,128)(2,1)S(1)} %constant_dynamic-update-slice_fusion.14, bf16[512,3072]{1,0:T(8,128)(2,1)S(1)} %copy-done.9, bf16[512,3072]{1,0:T(8,128)(2,1)S(1)} %copy-done.6), kind=kOutput, calls=%fused_computation.111 | convolution fusion | flops 9676259328 | bytes 22020096 | tf_op jit(solution)/shard_map/dot_general | solution.py:33
  812.9 13.8 %fusion.127 = f32[1024,1536]{1,0:T(8,128)} fusion(bf16[1024,3072]{1,0:T(8,128)(2,1)S(1)} %bitcast.29, bf16[1536,3072]{1,0:T(8,128)(2,1)} %constant_dynamic-update-slice_fusion.20), kind=kOutput, calls=%fused_computation.185 | convolution fusion | flops 9663676416 | bytes 22020096 | tf_op jit(solution)/shard_map/dot_general | solution.py:33
  826.7 21.9 %convolution_add_fusion = f32[1024,3072]{1,0:T(8,128)} fusion(f32[1024,3072]{1,0:T(8,128)} %convolution_add_fusion.2, bf16[1536,3072]{0,1:T(8,128)(2,1)} %copy-done.17, f32[1024,1536]{1,0:T(8,128)} %fusion.89, f32[1024,1536]{1,0:T(8,128)} %fusion.127), kind=kOutput, calls=%fused_computation.66 | convolution fusion | flops 9698279424 | bytes 47185920 | tf_op jit(solution)/shard_map/dot_general | solution.py:25
  851.8 20.0 %convolution_add_fusion.1 = f32[1024,3072]{1,0:T(8,128)} fusion(f32[1024,3072]{1,0:T(8,128)} %convolution_add_fusion.3, bf16[1536,3072]{1,0:T(8,128)(2,1)} %constant_dynamic-update-slice_fusion.20, f32[1024,1536]{1,0:T(8,128)} %fusion.89), kind=kOutput, calls=%fused_computation.67 | convolution fusion | flops 9680977920 | bytes 40894464 | tf_op jit(solution)/shard_map/dot_general | solution.py:25
  889.7 9.3 %fusion.25 = (bf16[512,3072]{1,0:T(8,128)(2,1)}, bf16[512,3072]{1,0:T(8,128)(2,1)}) fusion(bf16[512,3072]{1,0:T(8,128)(2,1)S(1)} %copy-done.1, bf16[512,3072]{1,0:T(8,128)(2,1)S(1)} %copy-done.4, f32[512,3072]{1,0:T(8,128)S(1)} %get-tuple-element.106, f32[512]{0:T(512)S(1)} %get-tuple-element.109, f32[512]{0:T(512)S(1)} %get-tuple-element.110, ...), kind=kLoop, calls=%fused_computation.37 | loop fusion | flops 22020096 | bytes 31477760 | tf_op jit(solution)/shard_map/convert_element_type | solution.py:126
  (178 shorter events, 166.3 us)
Async XLA Ops:
  7.2 232.3 %all-gather.3.cloned.1.call-start = ((), (), s32[]{:S(2)}) async-start(), calls=%async_computation | async-start | bytes 28311552 | tf_op jit(solution)/shard_map/all_gather | solution.py:84
  18.2 422.1 %all-gather.5.cloned.1.call-start = ((), (), s32[]{:S(2)}) async-start(), calls=%async_computation.1 | async-start | bytes 28311552 | tf_op jit(solution)/shard_map/all_gather | solution.py:86
  31.0 157.6 %collective-permute-start = (bf16[256,3072]{1,0:T(8,128)(2,1)}, bf16[256,3072]{1,0:T(8,128)(2,1)}, u32[]{:S(2)}, u32[]{:S(2)}) collective-permute-start(bf16[256,3072]{1,0:T(8,128)(2,1)} %constant_dynamic-slice_fusion.2), channel_id=1, source_target_pairs={{0,2},{1,3},{2,0},{3,1},{4,6},{5,7},{6,4},{7,5},{8,10},{9,11},{10,... | collective-permute-start | bytes 4718600 | tf_op jit(solution)/shard_map/ppermute | solution.py:37
  33.9 156.0 %collective-permute-start.1 = (bf16[256,3072]{1,0:T(8,128)(2,1)}, bf16[256,3072]{1,0:T(8,128)(2,1)}, u32[]{:S(2)}, u32[]{:S(2)}) collective-permute-start(bf16[256,3072]{1,0:T(8,128)(2,1)} %constant_dynamic-slice_fusion.2), channel_id=1, source_target_pairs={{0,4},{1,5},{2,6},{3,7},{4,0},{5,1},{6,2},{7,3},{8,12},{9,13},{10,... | collective-permute-start | bytes 4718600 | tf_op jit(solution)/shard_map/ppermute | solution.py:37
  35.4 128.9 %collective-permute-start.2 = (bf16[256,3072]{0,1:T(8,128)(2,1)}, bf16[256,3072]{0,1:T(8,128)(2,1)}, u32[]{:S(2)}, u32[]{:S(2)}) collective-permute-start(bf16[256,3072]{0,1:T(8,128)(2,1)} %dynamic-slice_bitcast_fusion), channel_id=1, source_target_pairs={{0,2},{1,3},{2,0},{3,1},{4,6},{5,7},{6,4},{7,5},{8,10},{9,11},{10,... | collective-permute-start | bytes 4718600 | tf_op jit(solution)/shard_map/ppermute | solution.py:37
  35.9 130.1 %collective-permute-start.3 = (bf16[256,3072]{0,1:T(8,128)(2,1)}, bf16[256,3072]{0,1:T(8,128)(2,1)}, u32[]{:S(2)}, u32[]{:S(2)}) collective-permute-start(bf16[256,3072]{0,1:T(8,128)(2,1)} %dynamic-slice_bitcast_fusion), channel_id=1, source_target_pairs={{0,4},{1,5},{2,6},{3,7},{4,0},{5,1},{6,2},{7,3},{8,12},{9,13},{10,... | collective-permute-start | bytes 4718600 | tf_op jit(solution)/shard_map/ppermute | solution.py:37
  41.0 279.6 %collective-permute-start.8 = (bf16[256,3072]{0,1:T(8,128)(2,1)}, bf16[256,3072]{0,1:T(8,128)(2,1)S(1)}, u32[]{:S(2)}, u32[]{:S(2)}) collective-permute-start(bf16[256,3072]{0,1:T(8,128)(2,1)} %constant_dynamic-slice_fusion.1), channel_id=1, source_target_pairs={{0,2},{1,3},{2,0},{3,1},{4,6},{5,7},{6,4},{7,5},{8,10},{9,11},{10,... | collective-permute-start | bytes 4718600 | tf_op jit(solution)/shard_map/ppermute | solution.py:37
  164.3 156.9 %collective-permute-start.9 = (bf16[256,3072]{0,1:T(8,128)(2,1)}, bf16[256,3072]{0,1:T(8,128)(2,1)S(1)}, u32[]{:S(2)}, u32[]{:S(2)}) collective-permute-start(bf16[256,3072]{0,1:T(8,128)(2,1)} %constant_dynamic-slice_fusion.1), channel_id=1, source_target_pairs={{0,4},{1,5},{2,6},{3,7},{4,0},{5,1},{6,2},{7,3},{8,12},{9,13},{10,... | collective-permute-start | bytes 4718600 | tf_op jit(solution)/shard_map/ppermute | solution.py:37
  166.0 118.2 %collective-permute-start.6 = (bf16[256,3072]{0,1:T(8,128)(2,1)}, bf16[256,3072]{0,1:T(8,128)(2,1)}, u32[]{:S(2)}, u32[]{:S(2)}) collective-permute-start(bf16[256,3072]{0,1:T(8,128)(2,1)} %collective-permute-done.3), channel_id=1, source_target_pairs={{0,2},{1,3},{2,0},{3,1},{4,6},{5,7},{6,4},{7,5},{8,10},{9,11},{10,... | collective-permute-start | bytes 4718600 | tf_op jit(solution)/shard_map/ppermute | solution.py:37
  188.5 157.0 %collective-permute-start.10 = (bf16[256,3072]{1,0:T(8,128)(2,1)}, bf16[256,3072]{1,0:T(8,128)(2,1)}, u32[]{:S(2)}, u32[]{:S(2)}) collective-permute-start(bf16[256,3072]{1,0:T(8,128)(2,1)} %constant_dynamic-slice_fusion), channel_id=1, source_target_pairs={{0,2},{1,3},{2,0},{3,1},{4,6},{5,7},{6,4},{7,5},{8,10},{9,11},{10,... | collective-permute-start | bytes 4718600 | tf_op jit(solution)/shard_map/ppermute | solution.py:37
  189.9 129.3 %collective-permute-start.7 = (bf16[256,3072]{1,0:T(8,128)(2,1)}, bf16[256,3072]{1,0:T(8,128)(2,1)}, u32[]{:S(2)}, u32[]{:S(2)}) collective-permute-start(bf16[256,3072]{1,0:T(8,128)(2,1)} %collective-permute-done), channel_id=1, source_target_pairs={{0,4},{1,5},{2,6},{3,7},{4,0},{5,1},{6,2},{7,3},{8,12},{9,13},{10,... | collective-permute-start | bytes 4718600 | tf_op jit(solution)/shard_map/ppermute | solution.py:37
  319.2 165.7 %collective-permute-start.12 = (bf16[256,3072]{0,1:T(8,128)(2,1)}, bf16[256,3072]{0,1:T(8,128)(2,1)}, u32[]{:S(2)}, u32[]{:S(2)}) collective-permute-start(bf16[256,3072]{0,1:T(8,128)(2,1)} %collective-permute-done.2), channel_id=1, source_target_pairs={{0,8},{8,0},{1,9},{9,1},{2,10},{10,2},{3,11},{11,3},{4,12},{12,4},... | collective-permute-start | bytes 4718600 | tf_op jit(solution)/shard_map/ppermute | solution.py:44
  320.7 209.2 %collective-permute-start.13 = (bf16[256,3072]{0,1:T(8,128)(2,1)}, bf16[256,3072]{0,1:T(8,128)(2,1)}, u32[]{:S(2)}, u32[]{:S(2)}) collective-permute-start(bf16[256,3072]{0,1:T(8,128)(2,1)} %collective-permute-done.3), channel_id=1, source_target_pairs={{0,8},{8,0},{1,9},{9,1},{2,10},{10,2},{3,11},{11,3},{4,12},{12,4},... | collective-permute-start | bytes 4718600 | tf_op jit(solution)/shard_map/ppermute | solution.py:44
  321.2 209.2 %collective-permute-start.14 = (bf16[256,3072]{1,0:T(8,128)(2,1)}, bf16[256,3072]{1,0:T(8,128)(2,1)}, u32[]{:S(2)}, u32[]{:S(2)}) collective-permute-start(bf16[256,3072]{1,0:T(8,128)(2,1)} %collective-permute-done), channel_id=1, source_target_pairs={{0,8},{8,0},{1,9},{9,1},{2,10},{10,2},{3,11},{11,3},{4,12},{12,4},... | collective-permute-start | bytes 4718600 | tf_op jit(solution)/shard_map/ppermute | solution.py:44
  346.7 136.1 %collective-permute-start.18 = (bf16[256,3072]{0,1:T(8,128)(2,1)S(1)}, bf16[256,3072]{0,1:T(8,128)(2,1)}, u32[]{:S(2)}, u32[]{:S(2)}) collective-permute-start(bf16[256,3072]{0,1:T(8,128)(2,1)S(1)} %collective-permute-done.9), channel_id=1, source_target_pairs={{0,2},{1,3},{2,0},{3,1},{4,6},{5,7},{6,4},{7,5},{8,10},{9,11},{10,... | collective-permute-start | bytes 4718600 | tf_op jit(solution)/shard_map/ppermute | solution.py:37
  348.3 136.0 %collective-permute-start.19 = (bf16[256,3072]{1,0:T(8,128)(2,1)}, bf16[256,3072]{1,0:T(8,128)(2,1)}, u32[]{:S(2)}, u32[]{:S(2)}) collective-permute-start(bf16[256,3072]{1,0:T(8,128)(2,1)} %collective-permute-done.10), channel_id=1, source_target_pairs={{0,4},{1,5},{2,6},{3,7},{4,0},{5,1},{6,2},{7,3},{8,12},{9,13},{10,... | collective-permute-start | bytes 4718600 | tf_op jit(solution)/shard_map/ppermute | solution.py:37
  484.3 69.8 %collective-permute-start.16 = (bf16[256,3072]{0,1:T(8,128)(2,1)}, bf16[256,3072]{0,1:T(8,128)(2,1)}, u32[]{:S(2)}, u32[]{:S(2)}) collective-permute-start(bf16[256,3072]{0,1:T(8,128)(2,1)} %collective-permute-done.6), channel_id=1, source_target_pairs={{0,8},{8,0},{1,9},{9,1},{2,10},{10,2},{3,11},{11,3},{4,12},{12,4},... | collective-permute-start | bytes 4718600 | tf_op jit(solution)/shard_map/ppermute | solution.py:44
  484.9 103.0 %collective-permute-start.17 = (bf16[256,3072]{1,0:T(8,128)(2,1)}, bf16[256,3072]{1,0:T(8,128)(2,1)}, u32[]{:S(2)}, u32[]{:S(2)}) collective-permute-start(bf16[256,3072]{1,0:T(8,128)(2,1)} %collective-permute-done.7), channel_id=1, source_target_pairs={{0,8},{8,0},{1,9},{9,1},{2,10},{10,2},{3,11},{11,3},{4,12},{12,4},... | collective-permute-start | bytes 4718600 | tf_op jit(solution)/shard_map/ppermute | solution.py:44
  529.8 145.6 %collective-permute-start.20 = (bf16[256,3072]{0,1:T(8,128)(2,1)}, bf16[256,3072]{0,1:T(8,128)(2,1)}, u32[]{:S(2)}, u32[]{:S(2)}) collective-permute-start(bf16[256,3072]{0,1:T(8,128)(2,1)} %copy-done.13), channel_id=1, source_target_pairs={{0,8},{8,0},{1,9},{9,1},{2,10},{10,2},{3,11},{11,3},{4,12},{12,4},... | collective-permute-start | bytes 4718600 | tf_op jit(solution)/shard_map/ppermute | solution.py:44
  530.4 183.8 %collective-permute-start.21 = (bf16[256,3072]{0,1:T(8,128)(2,1)}, bf16[256,3072]{0,1:T(8,128)(2,1)}, u32[]{:S(2)}, u32[]{:S(2)}) collective-permute-start(bf16[256,3072]{0,1:T(8,128)(2,1)} %copy-done.14), channel_id=1, source_target_pairs={{0,8},{8,0},{1,9},{9,1},{2,10},{10,2},{3,11},{11,3},{4,12},{12,4},... | collective-permute-start | bytes 4718600 | tf_op jit(solution)/shard_map/ppermute | solution.py:44
  531.9 182.3 %collective-permute-start.22 = (bf16[256,3072]{1,0:T(8,128)(2,1)}, bf16[256,3072]{1,0:T(8,128)(2,1)}, u32[]{:S(2)}, u32[]{:S(2)}) collective-permute-start(bf16[256,3072]{1,0:T(8,128)(2,1)} %collective-permute-done.10), channel_id=1, source_target_pairs={{0,8},{8,0},{1,9},{9,1},{2,10},{10,2},{3,11},{11,3},{4,12},{12,4},... | collective-permute-start | bytes 4718600 | tf_op jit(solution)/shard_map/ppermute | solution.py:44
  554.1 168.5 %collective-permute-start.23 = (bf16[256,3072]{1,0:T(8,128)(2,1)}, bf16[256,3072]{1,0:T(8,128)(2,1)}, u32[]{:S(2)}, u32[]{:S(2)}) collective-permute-start(bf16[256,3072]{1,0:T(8,128)(2,1)} %copy-done.15), channel_id=1, source_target_pairs={{0,8},{8,0},{1,9},{9,1},{2,10},{10,2},{3,11},{11,3},{4,12},{12,4},... | collective-permute-start | bytes 4718600 | tf_op jit(solution)/shard_map/ppermute | solution.py:44
  673.9 82.3 %collective-permute-start.24 = (bf16[256,3072]{0,1:T(8,128)(2,1)}, bf16[256,3072]{0,1:T(8,128)(2,1)S(1)}, u32[]{:S(2)}, u32[]{:S(2)}) collective-permute-start(bf16[256,3072]{0,1:T(8,128)(2,1)} %collective-permute-done.18), channel_id=1, source_target_pairs={{0,8},{8,0},{1,9},{9,1},{2,10},{10,2},{3,11},{11,3},{4,12},{12,4},... | collective-permute-start | bytes 4718600 | tf_op jit(solution)/shard_map/ppermute | solution.py:44
  675.4 113.9 %collective-permute-start.25 = (bf16[256,3072]{1,0:T(8,128)(2,1)}, bf16[256,3072]{1,0:T(8,128)(2,1)S(1)}, u32[]{:S(2)}, u32[]{:S(2)}) collective-permute-start(bf16[256,3072]{1,0:T(8,128)(2,1)} %collective-permute-done.19), channel_id=1, source_target_pairs={{0,8},{8,0},{1,9},{9,1},{2,10},{10,2},{3,11},{11,3},{4,12},{12,4},... | collective-permute-start | bytes 4718600 | tf_op jit(solution)/shard_map/ppermute | solution.py:44
  (42 other events, 838.0 us)
Sparse Core Ops, SparseCore 0:
  18.3 221.1 all-gather.2
  241.3 198.8 all-gather.4

commit v2 on v1

v2 whole, which is shorter than its diff:
```python
import functools
import math

import jax
import jax.numpy as jnp
from jax import lax
from jax.experimental import pallas as pl
from jax.experimental.pallas import tpu as pltpu
from jax.sharding import PartitionSpec as P


EPS = 1e-6
BF = jnp.bfloat16
F32 = jnp.float32


def _gelu(a):
    return jax.nn.gelu(a, approximate=True)


def _ln(x):
    mu = jnp.mean(x, axis=-1, keepdims=True)
    xc = x - mu
    var = jnp.mean(xc * xc, axis=-1, keepdims=True)
    rstd = lax.rsqrt(var + EPS)
    return xc * rstd, rstd


def _nn(a, b):
    return jnp.dot(a, b, preferred_element_type=F32)


def _tn(a, b):
    return lax.dot_general(a, b, (((0,), (0,)), ((), ())), preferred_element_type=F32)


def _nt(a, b):
    return lax.dot_general(a, b, (((1,), (1,)), ((), ())), preferred_element_type=F32)


def _swap(bit):
    return lambda v: lax.ppermute(v, "tp", [(i, i ^ bit) for i in range(8)])


CORE, XN, YN = _swap(1), _swap(2), _swap(4)


def ZN(v):
    return lax.ppermute(v, "data", [(0, 1), (1, 0)])


def _dact(A, dH):
    return jax.vjp(_gelu, A)[1](dH)[0].astype(BF)


def _cat(*v):
    return jnp.concatenate(v)


tie = lambda *v: lax.optimization_barrier(v)


ROWS = 512


def _mlp_kernel(steps, nw, acc, *refs):
    x_hbm, dy_hbm, w1s, w2s = refs[0], refs[1], refs[2:2 + nw], refs[2 + nw:2 + 2 * nw]
    refs = refs[2 + 2 * nw:]
    ins, refs = (refs[:4], refs[4:]) if acc else ((), refs)
    outs, (xb, yb, ya, da, w1b, w2b, wsem, xsem, asem, osem) = refs[:4], refs[4:]
    nb = len(steps)
    tiles = xb.shape[0] // ROWS
    width = xb.shape[1]

    def fetch(j, slot):
        at = 0
        for k, lo, r in steps[j]:
            pltpu.make_async_copy(w1s[k].at[:, pl.ds(lo, r)], w1b.at[slot, :, pl.ds(at, r)], wsem.at[0, slot]).start()
            pltpu.make_async_copy(w2s[k].at[pl.ds(lo, r)], w2b.at[slot, pl.ds(at, r)], wsem.at[1, slot]).start()
            at += r

    loads = [pltpu.make_async_copy(x_hbm, xb, xsem.at[0]), pltpu.make_async_copy(dy_hbm, yb, xsem.at[1])]
    sums = [(b, t) for b in (ya, da) for t in range(tiles)]
    fills = [pltpu.make_async_copy(r, b.at[pl.ds(t * ROWS, ROWS)], asem.at[i]) for i, (r, (b, t)) in enumerate(zip(ins, sums))]
    for c in loads:
        c.start()
    fetch(0, 0)
    for c in fills:
        c.start()
    if not acc:
        ya[...] = jnp.zeros_like(ya)
        da[...] = jnp.zeros_like(da)
    for c in loads:
        c.wait()
    for c in fills:
        c.wait()

    @pl.loop(0, nb)
    def _(j):
        slot = lax.rem(j, 2)
        pltpu.make_async_copy(w1b.at[slot], w1b.at[slot], wsem.at[0, slot]).wait()
        pltpu.make_async_copy(w2b.at[slot], w2b.at[slot], wsem.at[1, slot]).wait()
        for k in range(1, nb):
            @pl.when(j + 1 == k)
            def _():
                fetch(k, k % 2)

        @pl.loop(0, tiles)
        def _(t):
            m = pl.ds(pl.multiple_of(t * ROWS, ROWS), ROWS)
            a = jnp.dot(xb[m], w1b[slot], preferred_element_type=F32)
            dh = lax.dot_general(yb[m], w2b[slot], (((1,), (1,)), ((), ())), preferred_element_type=F32)
            c = math.sqrt(2 / math.pi)
            th = jnp.tanh(c * (a + 0.044715 * (a * a * a)))
            cdf = 0.5 * (1.0 + th)
            h = (a * cdf).astype(BF)
            d = (dh * (cdf + 0.5 * a * (1.0 - th * th) * (c * (1.0 + 3 * 0.044715 * (a * a))))).astype(BF)

            @pl.loop(0, width // ROWS)
            def _(i):
                n = pl.ds(pl.multiple_of(i * ROWS, ROWS), ROWS)
                ya[m, n] += jnp.dot(h, w2b[slot, :, n], preferred_element_type=F32)
                da[m, n] += lax.dot_general(d, w1b[slot, n], (((1,), (1,)), ((), ())), preferred_element_type=F32)

            for i, (b, tt) in enumerate(sums):
                @pl.when((j == nb - 1) & (t == tt))
                def _():
                    pltpu.make_async_copy(b.at[pl.ds(tt * ROWS, ROWS)], outs[i], osem.at[i]).start()

    for i, (b, tt) in enumerate(sums):
        pltpu.make_async_copy(b.at[pl.ds(tt * ROWS, ROWS)], outs[i], osem.at[i]).wait()


def mlp(x, dy, steps, w1s, w2s, sums=()):
    tokens, width = x.shape
    nw, nb = len(w1s), len(steps)
    hbm = pl.BlockSpec(memory_space=pl.ANY)
    return pl.pallas_call(
        functools.partial(_mlp_kernel, steps, nw, bool(sums)),
        out_shape=[jax.ShapeDtypeStruct((ROWS, width), F32)] * 4,
        in_specs=[hbm] * (2 + 2 * nw + len(sums)),
        out_specs=[hbm] * 4,
        scratch_shapes=[
            pltpu.VMEM((tokens, width), BF), pltpu.VMEM((tokens, width), BF),
            pltpu.VMEM((tokens, width), F32), pltpu.VMEM((tokens, width), F32),
            pltpu.VMEM((2, width, ROWS), BF), pltpu.VMEM((2, ROWS, width), BF),
            pltpu.SemaphoreType.DMA((2, 2)), pltpu.SemaphoreType.DMA((2,)),
            pltpu.SemaphoreType.DMA((4,)), pltpu.SemaphoreType.DMA((4,)),
        ],
        input_output_aliases={2 + 2 * nw + i: i for i in range(len(sums))},
        compiler_params=pltpu.CompilerParams(vmem_limit_bytes=63 * 1024 * 1024),
        cost_estimate=pl.CostEstimate(flops=8 * tokens * width * ROWS * nb, transcendentals=tokens * ROWS * nb,
                                      bytes_accessed=4 * width * ROWS * nb + 20 * tokens * width),
    )(x, dy, *w1s, *w2s, *sums)


def solution(mesh):
    rows = P(("data", "tp"), None)

    def block(X, gamma, W1, W2, dY):
        n = X.shape[0]
        zi = lax.axis_index("data")
        half = W2.shape[0] // 2
        q = half // 2

        def piece1(w, c):
            return lax.dynamic_slice_in_dim(w, zi * half + c * q, q, 1)

        def piece2(w, c):
            return lax.dynamic_slice_in_dim(w, zi * half + c * q, q, 0)

        Xp, dYp = CORE(X), CORE(dY)
        a1, a2 = piece1(W1, 0), piece2(W2, 0)
        x1, y1, x2, y2 = XN(a1), YN(a1), XN(a2), YN(a2)
        Xs, a1, a2 = tie(X, a1, a2)
        x = Xs.astype(F32)
        xhat, rstd = _ln(x)
        Xn = (xhat * gamma).astype(BF)
        m = n // 2
        gather = lambda v: lax.all_gather(v, "tp", axis=0, tiled=True)
        XaL, gL, XaH, gH = gather(Xn[:m]), gather(dY[:m]), gather(Xn[m:]), gather(dY[m:])
        W1s, W2s, Xn, Xp, dYp = tie(W1, W2, Xn, Xp, dYp)
        b1, b2 = piece1(W1s, 1), piece2(W2s, 1)
        bx1, by1, bx2, by2 = XN(b1), YN(b1), XN(b2), YN(b2)
        b1, b2, Xp = tie(b1, b2, Xp)
        Xnc = _cat(Xn, (_ln(Xp.astype(F32))[0] * gamma).astype(BF))
        dYc = _cat(dY, dYp)
        S = mlp(Xnc, dYc, [[(0, 0, ROWS)], [(0, ROWS, ROWS)]], [W1], [W2])
        x1, y1, x2, y2, *S = tie(x1, y1, x2, y2, *S)
        zx1, zy1, d1 = ZN(x1), ZN(y1), XN(y1)
        zx2, zy2, d2 = ZN(x2), ZN(y2), YN(x2)
        pair = lambda k: [(k, 0, q), (k + 1, 0, q)]
        S = mlp(Xnc, dYc, [pair(0)], [x1, y1], [x2, y2], S)
        XaL, *S = tie(XaL, *S)
        AL = _nn(XaL, W1)
        gL, bx1, by1, bx2, by2, AL = tie(gL, bx1, by1, bx2, by2, AL)
        bzx1, bzy1, bzx2, bzy2 = ZN(bx1), ZN(by1), ZN(bx2), ZN(by2)
        bd1, bd2 = XN(by1), YN(bx2)
        dAL = _dact(AL, _nt(gL, W2))
        d1, d2, dAL = tie(d1, d2, dAL)
        zd1, zd2 = ZN(d1), ZN(d2)
        dW2, dW1 = _tn(_gelu(AL).astype(BF), gL), _tn(XaL, dAL)
        zx1, zy1, zx2, zy2, dW2, dW1, *S = tie(zx1, zy1, zx2, zy2, dW2, dW1, *S)
        S = mlp(Xnc, dYc, [pair(0), pair(2)], [bx1, by1, zx1, zy1], [bx2, by2, zx2, zy2], S)
        XaH, bd1, bd2, *S = tie(XaH, bd1, bd2, *S)
        bzd1, bzd2 = ZN(bd1), ZN(bd2)
        AH = _nn(XaH, W1)
        gH, AH, dW2, dW1 = tie(gH, AH, dW2, dW1)
        dAH = _dact(AH, _nt(gH, W2))
        dW2, dW1 = dW2 + _tn(_gelu(AH).astype(BF), gH), dW1 + _tn(XaH, dAH)
        bzx1, bzy1, bzx2, bzy2, zd1, zd2, dW2, dW1, *S = tie(bzx1, bzy1, bzx2, bzy2, zd1, zd2, dW2, dW1, *S)
        S = mlp(Xnc, dYc, [pair(0), pair(2)], [bzx1, bzy1, d1, zd1], [bzx2, bzy2, d2, zd2], S)
        bzd1, bzd2, *S = tie(bzd1, bzd2, *S)
        Yo, Yp, dXo, dXp = mlp(Xnc, dYc, [pair(0)], [bd1, bzd1], [bd2, bzd2], S)

        dXn = dXo + CORE(dXp)
        Y = (x + (Yo + CORE(Yp))).astype(BF)
        dgamma = jnp.sum(dXn * xhat, axis=0)
        for hop in (CORE, XN, YN):
            dgamma = dgamma + hop(dgamma)
        dxhat = dXn * gamma
        dx = rstd * (dxhat - jnp.mean(dxhat, axis=-1, keepdims=True) - xhat * jnp.mean(dxhat * xhat, axis=-1, keepdims=True))
        dX = (dY.astype(F32) + dx).astype(BF)
        return Y, dX, dW1, dW2, dgamma

    return jax.shard_map(block, mesh=mesh,
                         in_specs=(rows, P(None), P(None, "tp"), P("tp", None), rows),
                         out_specs=(rows, rows, P("data", "tp"), rows, P("data")),
                         check_vma=False)
```

time: 910 us -> 716 us (0.79)
  Pallas kernels: 0 us -> 210 us
  waiting for transfers between devices: 423 us -> 214 us
  matrix products: 332 us -> 175 us
  local copies, waits for them, and re-layouts: 80.6 us -> 26.2 us
    pallas_call x0 -> x5, Pallas kernels: none -> 210 us  [mlp(): pl.pallas_call(functools.partial(_mlp_kernel, steps, nw, bool(sums)), out...]
    all_gather x2 -> x4, waiting for transfers between devices: 118 us -> 13.9 us  [block(): gather = lambda v: lax.all_gather(v, 'tp', axis=0, tiled=True)]
    dot_general x7 -> x2, matrix products: 137 us -> 38.5 us  [_nn(): return jnp.dot(a, b, preferred_element_type=F32)]
    ppermute x12, waiting for transfers between devices: 129 us -> 50.6 us  [ZN(): return lax.ppermute(v, 'data', [(0, 1), (1, 0)])]
    dot_general x7 -> x2, matrix products: 118 us -> 46 us  [_nt(): lax.dot_general(a, b, (((1,), (1,)), ((), ())), preferred_element_type=F32)]
    unnamed x87 -> x33, local copies, waits for them, and re-layouts: 56.1 us -> 5.95 us
    ppermute x19, waiting for transfers between devices: 176 us -> 149 us  [_swap(): return lambda v: lax.ppermute(v, 'tp', [(i, i ^ bit) for i in range(8)])]
    dot_general x2 -> x4, matrix products: 77.3 us -> 90.5 us  [_tn(): lax.dot_general(a, b, (((0,), (0,)), ((), ())), preferred_element_type=F32)]
  transfers between devices with their start and end apart: 33 -> 35, of which waited for: 15 -> 14; matrix products, arithmetic and copies ran while one was open for 39% -> 31% of each run, Pallas kernels for 0% -> 25%
where the time goes in v2:
time: 716 us; the launch traced here: 709 us
  waiting for transfers between devices  214 us (30%)
  Pallas kernels  210 us (29%)
  matrix products  175 us (24%)
  starting transfers between devices  38.8 us (5%)
  other arithmetic  29.9 us (4%)
  local copies, waits for them, and re-layouts  26.2 us (4%)
  between operations  14.3 us (2%)
    pallas_call x5, Pallas kernels, mlp(): pl.pallas_call(functools.partial(_mlp_kernel, steps, nw, bool(sums)), out...  210 us
    ppermute x19, waiting for transfers between devices, _swap(): return lambda v: lax.ppermute(v, 'tp', [(i, i ^ bit) for i in range(8)])  149 us
    dot_general x4, matrix products, _tn(): lax.dot_general(a, b, (((0,), (0,)), ((), ())), preferred_element_type=F32)  90.5 us
    ppermute x12, waiting for transfers between devices, ZN(): return lax.ppermute(v, 'data', [(0, 1), (1, 0)])  50.6 us
    dot_general x2, matrix products, _nt(): lax.dot_general(a, b, (((1,), (1,)), ((), ())), preferred_element_type=F32)  46 us
    dot_general x2, matrix products, _nn(): return jnp.dot(a, b, preferred_element_type=F32)  38.5 us
    ppermute x19, starting transfers between devices, _swap(): return lambda v: lax.ppermute(v, 'tp', [(i, i ^ bit) for i in range(8)])  24.1 us
    ppermute x12, starting transfers between devices, ZN(): return lax.ppermute(v, 'data', [(0, 1), (1, 0)])  14.6 us
  transfers between devices with their start and end apart: 35, of which 14 were waited for; matrix products, arithmetic and copies ran while one was open for 31% of the time, Pallas kernels for 25%

profile of v2, /device:TPU:0, one launch (start us, length us, event | category | flops | bytes accessed | tf_op | source)
XLA Modules:
  0.0 708.7 jit_solution(2610861036918797035)
XLA Ops:
  29.9 4.2 constant_dynamic-update-slice_fusion.1
  58.6 42.3 %shard_map.92 = (f32[512,3072]{1,0:T(8,128)}, f32[512,3072]{1,0:T(8,128)}, f32[512,3072]{1,0:T(8,128)}, f32[512,3072]{1,0:T(8,128)}) custom-call(bf16[1024,3072]{1,0:T(8,128)(2,1)} %pad_maximum_fusion.refs_0_, bf16[1024,3072]{1,0:T(8,128)(2,1)} %constant_dynamic-update-slice_fusion.refs_1_, bf16[3072,1024]{1,0:T(8,128)(2,1)} %refs_2_.1, ...), custom_call_target="tpu_custom_call" | custom-call | flops 25769803776 | bytes 75497472 | tf_op jit(solution)/shard_map/pallas_call | solution.py:138
  103.0 44.6 %collective-permute-done.8.refs_4_ = bf16[256,3072]{1,0:T(8,128)(2,1)} collective-permute-done((bf16[256,3072]{1,0:T(8,128)(2,1)}, bf16[256,3072]{1,0:T(8,128)(2,1)}, u32[]{:S(2)}, u32[]{:S(2)}) %collective-permute-start.8) | collective-permute-done | bytes 1572896 | tf_op jit(solution)/shard_map/ppermute | solution.py:42
  151.3 34.0 %shard_map.93 = (f32[512,3072]{1,0:T(8,128)}, f32[512,3072]{1,0:T(8,128)}, f32[512,3072]{1,0:T(8,128)}, f32[512,3072]{1,0:T(8,128)}) custom-call(bf16[1024,3072]{1,0:T(8,128)(2,1)} %pad_maximum_fusion.refs_0_, bf16[1024,3072]{1,0:T(8,128)(2,1)} %constant_dynamic-update-slice_fusion.refs_1_, ...), custom_call_target="tpu_custom_call", output_to_operand_aliasing={{0}: (6, {}), {1}: (7, {}), {2}: (8, {}), {3}: (9, {})} | custom-call | flops 12884901888 | bytes 69206016 | tf_op jit(solution)/shard_map/pallas_call | solution.py:138
  185.3 19.2 %fusion.66 = f32[2048,1024]{1,0:T(8,128)} fusion(bf16[2048,3072]{1,0:T(8,128)(2,1)} %all-gather.9.cloned.1.call-done, bf16[3072,1024]{1,0:T(8,128)(2,1)} %refs_2_.1), kind=kOutput, calls=%fused_computation.92 | convolution fusion | flops 12884901888 | bytes 27262976 | tf_op jit(solution)/shard_map/dot_general | solution.py:30
  209.5 55.5 %collective-permute-done.4.refs_6_ = bf16[256,3072]{1,0:T(8,128)(2,1)} collective-permute-done((bf16[256,3072]{1,0:T(8,128)(2,1)}, bf16[256,3072]{1,0:T(8,128)(2,1)}, u32[]{:S(2)}, u32[]{:S(2)}) %collective-permute-start.4) | collective-permute-done | bytes 1572896 | tf_op jit(solution)/shard_map/ppermute | solution.py:42
  268.2 26.3 %fusion.6 = bf16[2048,1024]{1,0:T(8,128)(2,1)} fusion(f32[2048,1024]{1,0:T(8,128)} %fusion.66, bf16[2048,3072]{1,0:T(8,128)(2,1)} %all-gather.7.cloned.1.call-done, bf16[1024,3072]{1,0:T(8,128)(2,1)} %refs_3_.1), kind=kOutput, calls=%fused_computation.13 | convolution fusion | flops 12926844928 | bytes 31457280 | tf_op jit(solution)/shard_map/dot_general | solution.py:38
  294.5 30.1 %collective-permute-done.16.refs_4_ = bf16[3072,256]{1,0:T(8,128)(2,1)S(1)} collective-permute-done((bf16[3072,256]{1,0:T(8,128)(2,1)}, bf16[3072,256]{1,0:T(8,128)(2,1)S(1)}, u32[]{:S(2)}, u32[]{:S(2)}) %collective-permute-start.16) | collective-permute-done | bytes 1572896 | tf_op jit(solution)/shard_map/ppermute | solution.py:42
  328.7 19.3 %fusion.67 = f32[3072,1024]{1,0:T(8,128)} fusion(bf16[2048,3072]{1,0:T(8,128)(2,1)} %all-gather.9.cloned.1.call-done, bf16[2048,1024]{1,0:T(8,128)(2,1)} %fusion.6), kind=kOutput, calls=%fused_computation.93 | convolution fusion | flops 12884901888 | bytes 29360128 | tf_op jit(solution)/shard_map/dot_general | solution.py:34
  348.0 18.8 %fusion.34 = f32[1024,3072]{1,0:T(8,128)} fusion(bf16[2048,3072]{1,0:T(8,128)(2,1)S(1)} %copy-done.11, f32[2048,1024]{1,0:T(8,128)S(1)} %copy-done.15), kind=kOutput, calls=%fused_computation.49 | convolution fusion | flops 12903776256 | bytes 33554432 | tf_op jit(solution)/shard_map/dot_general | solution.py:34
  371.6 50.7 %shard_map.94 = (f32[512,3072]{1,0:T(8,128)}, f32[512,3072]{1,0:T(8,128)}, f32[512,3072]{1,0:T(8,128)}, f32[512,3072]{1,0:T(8,128)}) custom-call(bf16[1024,3072]{1,0:T(8,128)(2,1)} %pad_maximum_fusion.refs_0_, ...), custom_call_target="tpu_custom_call", output_to_operand_aliasing={{0}: (10, {}), {1}: (11, {}), {2}: (12, {}), {3}: (13, {})} | custom-call | flops 25769803776 | bytes 75497472 | tf_op jit(solution)/shard_map/pallas_call | solution.py:138
  424.4 19.3 %fusion.68 = f32[2048,1024]{1,0:T(8,128)} fusion(bf16[2048,3072]{1,0:T(8,128)(2,1)} %all-gather.5.cloned.1.call-done, bf16[3072,1024]{1,0:T(8,128)(2,1)} %refs_2_.1), kind=kOutput, calls=%fused_computation.94 | convolution fusion | flops 12884901888 | bytes 27262976 | tf_op jit(solution)/shard_map/dot_general | solution.py:30
  443.7 13.8 %all-gather.11.cloned.1.call-done = bf16[2048,3072]{1,0:T(8,128)(2,1)} async-done(((bf16[256,3072]{1,0:T(8,128)(2,1)}), bf16[2048,3072]{1,0:T(8,128)(2,1)}) %all-gather.11.cloned.1.call-update) | async-done | bytes 12582928 | tf_op jit(solution)/shard_map/all_gather | solution.py:180
  457.5 19.8 %fusion.69 = f32[2048,1024]{1,0:T(8,128)} fusion(bf16[2048,3072]{1,0:T(8,128)(2,1)} %all-gather.11.cloned.1.call-done, bf16[1024,3072]{1,0:T(8,128)(2,1)} %refs_3_.1), kind=kOutput, calls=%fused_computation.95 | convolution fusion | flops 12884901888 | bytes 27262976 | tf_op jit(solution)/shard_map/dot_general | solution.py:38
  477.3 27.0 %convolution_add_fusion = f32[3072,1024]{1,0:T(8,128)} fusion(f32[3072,1024]{1,0:T(8,128)} %fusion.67, bf16[2048,3072]{1,0:T(8,128)(2,1)} %all-gather.5.cloned.1.call-done, f32[2048,1024]{1,0:T(8,128)} %fusion.68, f32[2048,1024]{1,0:T(8,128)} %fusion.69), kind=kOutput, calls=%fused_computation.33 | convolution fusion | flops 12929990656 | bytes 54525952 | tf_op jit(solution)/shard_map/dot_general | solution.py:34
  505.8 25.4 %convolution_add_fusion.1 = f32[1024,3072]{1,0:T(8,128)} fusion(f32[1024,3072]{1,0:T(8,128)} %fusion.34, bf16[2048,3072]{1,0:T(8,128)(2,1)} %all-gather.11.cloned.1.call-done, f32[2048,1024]{1,0:T(8,128)} %fusion.68), kind=kOutput, calls=%fused_computation.34 | convolution fusion | flops 12906921984 | bytes 46137344 | tf_op jit(solution)/shard_map/dot_general | solution.py:34
  533.2 5.9 collective-permute-done.24.refs_5_
  539.2 33.7 %collective-permute-done.25.refs_9_ = bf16[256,3072]{1,0:T(8,128)(2,1)} collective-permute-done((bf16[256,3072]{1,0:T(8,128)(2,1)S(1)}, bf16[256,3072]{1,0:T(8,128)(2,1)}, u32[]{:S(2)}, u32[]{:S(2)}) %collective-permute-start.25) | collective-permute-done | bytes 1572896 | tf_op jit(solution)/shard_map/ppermute | solution.py:49
  572.9 49.3 %shard_map.95 = (f32[512,3072]{1,0:T(8,128)}, f32[512,3072]{1,0:T(8,128)}, f32[512,3072]{1,0:T(8,128)}, f32[512,3072]{1,0:T(8,128)}) custom-call(bf16[1024,3072]{1,0:T(8,128)(2,1)} %pad_maximum_fusion.refs_0_, ...), custom_call_target="tpu_custom_call", output_to_operand_aliasing={{0}: (10, {}), {1}: (11, {}), {2}: (12, {}), {3}: (13, {})} | custom-call | flops 25769803776 | bytes 75497472 | tf_op jit(solution)/shard_map/pallas_call | solution.py:138
  622.2 10.9 %collective-permute-done.19.refs_5_ = bf16[256,3072]{1,0:T(8,128)(2,1)} collective-permute-done((bf16[256,3072]{1,0:T(8,128)(2,1)}, bf16[256,3072]{1,0:T(8,128)(2,1)}, u32[]{:S(2)}, u32[]{:S(2)}) %collective-permute-start.19) | collective-permute-done | bytes 1572896 | tf_op jit(solution)/shard_map/ppermute | solution.py:49
  633.1 34.1 %shard_map.96 = (f32[512,3072]{1,0:T(8,128)}, f32[512,3072]{1,0:T(8,128)}, f32[512,3072]{1,0:T(8,128)}, f32[512,3072]{1,0:T(8,128)}) custom-call(bf16[1024,3072]{1,0:T(8,128)(2,1)} %pad_maximum_fusion.refs_0_, bf16[1024,3072]{1,0:T(8,128)(2,1)} %constant_dynamic-update-slice_fusion.refs_1_, ...), custom_call_target="tpu_custom_call", output_to_operand_aliasing={{0}: (6, {}), {1}: (7, {}), {2}: (8, {}), {3}: (9, {})} | custom-call | flops 12884901888 | bytes 69206016 | tf_op jit(solution)/shard_map/pallas_call | solution.py:138
  667.8 9.9 %collective-permute-done.27 = f32[512,3072]{1,0:T(8,128)S(1)} collective-permute-done((f32[512,3072]{1,0:T(8,128)}, f32[512,3072]{1,0:T(8,128)S(1)}, u32[]{:S(2)}, u32[]{:S(2)}) %collective-permute-start.27) | collective-permute-done | bytes 6291488 | tf_op jit(solution)/shard_map/ppermute | solution.py:42
  677.7 5.8 fusion.28
  692.8 8.5 %fusion.27 = (bf16[512,3072]{1,0:T(8,128)(2,1)}, bf16[512,3072]{1,0:T(8,128)(2,1)}) fusion(bf16[512,3072]{1,0:T(8,128)(2,1)S(1)} %copy-done.1, bf16[512,3072]{1,0:T(8,128)(2,1)S(1)} %copy-done.4, f32[512,3072]{1,0:T(8,128)S(1)} %get-tuple-element.184, f32[512]{0:T(512)S(1)} %get-tuple-element.191, f32[512]{0:T(512)S(1)} %get-tuple-element.192, ...), kind=kLoop, calls=%fused_computation.40 | loop fusion | flops 22020096 | bytes 31477760 | tf_op jit(solution)/shard_map/convert_element_type | solution.py:223
  (120 shorter events, 86.1 us)
Async XLA Ops:
  7.2 178.1 %all-gather.9.cloned.1.call-start = ((), (), s32[]{:S(2)}) async-start(), calls=%async_computation.2 | async-start | bytes 14155776 | tf_op jit(solution)/shard_map/all_gather | solution.py:180
  19.4 248.8 %all-gather.7.cloned.1.call-start = ((), (), s32[]{:S(2)}) async-start(), calls=%async_computation.1 | async-start | bytes 14155776 | tf_op jit(solution)/shard_map/all_gather | solution.py:180
  23.3 401.1 %all-gather.5.cloned.1.call-start = ((), (), s32[]{:S(2)}) async-start(), calls=%async_computation | async-start | bytes 14155776 | tf_op jit(solution)/shard_map/all_gather | solution.py:180
  24.0 433.5 %all-gather.11.cloned.1.call-start = ((), (), s32[]{:S(2)}) async-start(), calls=%async_computation.3 | async-start | bytes 14155776 | tf_op jit(solution)/shard_map/all_gather | solution.py:180
  24.9 76.1 %collective-permute-start.6 = (bf16[3072,256]{1,0:T(8,128)(2,1)}, bf16[3072,256]{1,0:T(8,128)(2,1)}, u32[]{:S(2)}, u32[]{:S(2)}) collective-permute-start(bf16[3072,256]{1,0:T(8,128)(2,1)} %constant_dynamic-slice_fusion.3), channel_id=1, source_target_pairs={{0,2},{1,3},{2,0},{3,1},{4,6},{5,7},{6,4},{7,5},{8,10},{9,11},{10,... | collective-permute-start | bytes 4718600 | tf_op jit(solution)/shard_map/ppermute | solution.py:42
  27.8 74.7 %collective-permute-start.7 = (bf16[3072,256]{1,0:T(8,128)(2,1)}, bf16[3072,256]{1,0:T(8,128)(2,1)}, u32[]{:S(2)}, u32[]{:S(2)}) collective-permute-start(bf16[3072,256]{1,0:T(8,128)(2,1)} %constant_dynamic-slice_fusion.3), channel_id=1, source_target_pairs={{0,4},{1,5},{2,6},{3,7},{4,0},{5,1},{6,2},{7,3},{8,12},{9,13},{10,... | collective-permute-start | bytes 4718600 | tf_op jit(solution)/shard_map/ppermute | solution.py:42
  29.3 118.3 %collective-permute-start.8 = (bf16[256,3072]{1,0:T(8,128)(2,1)}, bf16[256,3072]{1,0:T(8,128)(2,1)}, u32[]{:S(2)}, u32[]{:S(2)}) collective-permute-start(bf16[256,3072]{1,0:T(8,128)(2,1)} %constant_dynamic-slice_fusion.2), channel_id=1, source_target_pairs={{0,2},{1,3},{2,0},{3,1},{4,6},{5,7},{6,4},{7,5},{8,10},{9,11},{10,... | collective-permute-start | bytes 4718600 | tf_op jit(solution)/shard_map/ppermute | solution.py:42
  34.1 115.6 %collective-permute-start.9 = (bf16[256,3072]{1,0:T(8,128)(2,1)}, bf16[256,3072]{1,0:T(8,128)(2,1)}, u32[]{:S(2)}, u32[]{:S(2)}) collective-permute-start(bf16[256,3072]{1,0:T(8,128)(2,1)} %constant_dynamic-slice_fusion.2), channel_id=1, source_target_pairs={{0,4},{1,5},{2,6},{3,7},{4,0},{5,1},{6,2},{7,3},{8,12},{9,13},{10,... | collective-permute-start | bytes 4718600 | tf_op jit(solution)/shard_map/ppermute | solution.py:42
  40.1 165.0 %collective-permute-start.2 = (bf16[3072,256]{1,0:T(8,128)(2,1)}, bf16[3072,256]{1,0:T(8,128)(2,1)}, u32[]{:S(2)}, u32[]{:S(2)}) collective-permute-start(bf16[3072,256]{1,0:T(8,128)(2,1)} %constant_dynamic-slice_fusion.1), channel_id=1, source_target_pairs={{0,2},{1,3},{2,0},{3,1},{4,6},{5,7},{6,4},{7,5},{8,10},{9,11},{10,... | collective-permute-start | bytes 4718600 | tf_op jit(solution)/shard_map/ppermute | solution.py:42
  101.0 106.8 %collective-permute-start.3 = (bf16[3072,256]{1,0:T(8,128)(2,1)}, bf16[3072,256]{1,0:T(8,128)(2,1)}, u32[]{:S(2)}, u32[]{:S(2)}) collective-permute-start(bf16[3072,256]{1,0:T(8,128)(2,1)} %constant_dynamic-slice_fusion.1), channel_id=1, source_target_pairs={{0,4},{1,5},{2,6},{3,7},{4,0},{5,1},{6,2},{7,3},{8,12},{9,13},{10,... | collective-permute-start | bytes 4718600 | tf_op jit(solution)/shard_map/ppermute | solution.py:42
  102.5 162.5 %collective-permute-start.4 = (bf16[256,3072]{1,0:T(8,128)(2,1)}, bf16[256,3072]{1,0:T(8,128)(2,1)}, u32[]{:S(2)}, u32[]{:S(2)}) collective-permute-start(bf16[256,3072]{1,0:T(8,128)(2,1)} %constant_dynamic-slice_fusion), channel_id=1, source_target_pairs={{0,2},{1,3},{2,0},{3,1},{4,6},{5,7},{6,4},{7,5},{8,10},{9,11},{10,... | collective-permute-start | bytes 4718600 | tf_op jit(solution)/shard_map/ppermute | solution.py:42
  147.6 119.1 %collective-permute-start.5 = (bf16[256,3072]{1,0:T(8,128)(2,1)}, bf16[256,3072]{1,0:T(8,128)(2,1)}, u32[]{:S(2)}, u32[]{:S(2)}) collective-permute-start(bf16[256,3072]{1,0:T(8,128)(2,1)} %constant_dynamic-slice_fusion), channel_id=1, source_target_pairs={{0,4},{1,5},{2,6},{3,7},{4,0},{5,1},{6,2},{7,3},{8,12},{9,13},{10,... | collective-permute-start | bytes 4718600 | tf_op jit(solution)/shard_map/ppermute | solution.py:42
  149.7 217.1 %collective-permute-start.12 = (bf16[3072,256]{1,0:T(8,128)(2,1)}, bf16[3072,256]{1,0:T(8,128)(2,1)}, u32[]{:S(2)}, u32[]{:S(2)}) collective-permute-start(bf16[3072,256]{1,0:T(8,128)(2,1)} %collective-permute-done.6.refs_2_), channel_id=1, source_target_pairs={{0,8},{8,0},{1,9},{9,1},{2,10},{10,2},{3,11},{11,3},{4,12},{12,4},... | collective-permute-start | bytes 4718600 | tf_op jit(solution)/shard_map/ppermute | solution.py:49
  205.0 162.3 %collective-permute-start.13 = (bf16[3072,256]{1,0:T(8,128)(2,1)}, bf16[3072,256]{1,0:T(8,128)(2,1)}, u32[]{:S(2)}, u32[]{:S(2)}) collective-permute-start(bf16[3072,256]{1,0:T(8,128)(2,1)} %collective-permute-done.7.refs_3_), channel_id=1, source_target_pairs={{0,8},{8,0},{1,9},{9,1},{2,10},{10,2},{3,11},{11,3},{4,12},{12,4},... | collective-permute-start | bytes 4718600 | tf_op jit(solution)/shard_map/ppermute | solution.py:49
  207.8 161.8 %collective-permute-start.14 = (bf16[256,3072]{1,0:T(8,128)(2,1)}, bf16[256,3072]{1,0:T(8,128)(2,1)}, u32[]{:S(2)}, u32[]{:S(2)}) collective-permute-start(bf16[256,3072]{1,0:T(8,128)(2,1)} %collective-permute-done.8.refs_4_), channel_id=1, source_target_pairs={{0,8},{8,0},{1,9},{9,1},{2,10},{10,2},{3,11},{11,3},{4,12},{12,4},... | collective-permute-start | bytes 4718600 | tf_op jit(solution)/shard_map/ppermute | solution.py:49
  327.2 95.1 %collective-permute-start.10 = (bf16[3072,256]{1,0:T(8,128)(2,1)}, bf16[3072,256]{1,0:T(8,128)(2,1)}, u32[]{:S(2)}, u32[]{:S(2)}) collective-permute-start(bf16[3072,256]{1,0:T(8,128)(2,1)} %collective-permute-done.3.refs_3_), channel_id=1, source_target_pairs={{0,2},{1,3},{2,0},{3,1},{4,6},{5,7},{6,4},{7,5},{8,10},{9,11},{10,... | collective-permute-start | bytes 4718600 | tf_op jit(solution)/shard_map/ppermute | solution.py:42
  366.8 164.4 %collective-permute-start.21 = (bf16[3072,256]{1,0:T(8,128)(2,1)}, bf16[3072,256]{1,0:T(8,128)(2,1)}, u32[]{:S(2)}, u32[]{:S(2)}) collective-permute-start(bf16[3072,256]{1,0:T(8,128)(2,1)} %collective-permute-done.3.refs_3_), channel_id=1, source_target_pairs={{0,8},{8,0},{1,9},{9,1},{2,10},{10,2},{3,11},{11,3},{4,12},{12,4},... | collective-permute-start | bytes 4718600 | tf_op jit(solution)/shard_map/ppermute | solution.py:49
  369.6 162.2 %collective-permute-start.22 = (bf16[256,3072]{1,0:T(8,128)(2,1)}, bf16[256,3072]{1,0:T(8,128)(2,1)}, u32[]{:S(2)}, u32[]{:S(2)}) collective-permute-start(bf16[256,3072]{1,0:T(8,128)(2,1)} %collective-permute-done.4.refs_6_), channel_id=1, source_target_pairs={{0,8},{8,0},{1,9},{9,1},{2,10},{10,2},{3,11},{11,3},{4,12},{12,4},... | collective-permute-start | bytes 4718600 | tf_op jit(solution)/shard_map/ppermute | solution.py:49
  370.3 134.0 %collective-permute-start.20 = (bf16[3072,256]{1,0:T(8,128)(2,1)}, bf16[3072,256]{1,0:T(8,128)(2,1)}, u32[]{:S(2)}, u32[]{:S(2)}) collective-permute-start(bf16[3072,256]{1,0:T(8,128)(2,1)} %collective-permute-done.2.refs_2_), channel_id=1, source_target_pairs={{0,8},{8,0},{1,9},{9,1},{2,10},{10,2},{3,11},{11,3},{4,12},{12,4},... | collective-permute-start | bytes 4718600 | tf_op jit(solution)/shard_map/ppermute | solution.py:49
  422.3 110.9 %collective-permute-start.23 = (bf16[256,3072]{1,0:T(8,128)(2,1)}, bf16[256,3072]{1,0:T(8,128)(2,1)}, u32[]{:S(2)}, u32[]{:S(2)}) collective-permute-start(bf16[256,3072]{1,0:T(8,128)(2,1)} %collective-permute-done.5.refs_7_), channel_id=1, source_target_pairs={{0,8},{8,0},{1,9},{9,1},{2,10},{10,2},{3,11},{11,3},{4,12},{12,4},... | collective-permute-start | bytes 4718600 | tf_op jit(solution)/shard_map/ppermute | solution.py:49
  422.4 116.8 %collective-permute-start.24 = (bf16[3072,256]{1,0:T(8,128)(2,1)}, bf16[3072,256]{1,0:T(8,128)(2,1)}, u32[]{:S(2)}, u32[]{:S(2)}) collective-permute-start(bf16[3072,256]{1,0:T(8,128)(2,1)} %copy-done.12), channel_id=1, source_target_pairs={{0,8},{8,0},{1,9},{9,1},{2,10},{10,2},{3,11},{11,3},{4,12},{12,4},... | collective-permute-start | bytes 4718600 | tf_op jit(solution)/shard_map/ppermute | solution.py:49
  504.3 68.6 %collective-permute-start.25 = (bf16[256,3072]{1,0:T(8,128)(2,1)S(1)}, bf16[256,3072]{1,0:T(8,128)(2,1)}, u32[]{:S(2)}, u32[]{:S(2)}) collective-permute-start(bf16[256,3072]{1,0:T(8,128)(2,1)S(1)} %copy-done.14), channel_id=1, source_target_pairs={{0,8},{8,0},{1,9},{9,1},{2,10},{10,2},{3,11},{11,3},{4,12},{12,4},... | collective-permute-start | bytes 4718600 | tf_op jit(solution)/shard_map/ppermute | solution.py:49
  531.2 91.0 %collective-permute-start.18 = (bf16[3072,256]{1,0:T(8,128)(2,1)}, bf16[3072,256]{1,0:T(8,128)(2,1)}, u32[]{:S(2)}, u32[]{:S(2)}) collective-permute-start(bf16[3072,256]{1,0:T(8,128)(2,1)} %collective-permute-done.10.refs_2_), channel_id=1, source_target_pairs={{0,8},{8,0},{1,9},{9,1},{2,10},{10,2},{3,11},{11,3},{4,12},{12,4},... | collective-permute-start | bytes 4718600 | tf_op jit(solution)/shard_map/ppermute | solution.py:49
  531.8 101.3 %collective-permute-start.19 = (bf16[256,3072]{1,0:T(8,128)(2,1)}, bf16[256,3072]{1,0:T(8,128)(2,1)}, u32[]{:S(2)}, u32[]{:S(2)}) collective-permute-start(bf16[256,3072]{1,0:T(8,128)(2,1)} %collective-permute-done.11.refs_4_), channel_id=1, source_target_pairs={{0,8},{8,0},{1,9},{9,1},{2,10},{10,2},{3,11},{11,3},{4,12},{12,4},... | collective-permute-start | bytes 4718600 | tf_op jit(solution)/shard_map/ppermute | solution.py:49
  (27 other events, 669.6 us)
Sparse Core Ops, SparseCore 0:
  19.5 121.7 all-gather.8
  143.2 118.9 all-gather.6
  264.1 113.7 all-gather.4
  379.6 77.8 all-gather.10
